TPU v7x, 128 devices: a whole 4x4x4 slice. The times are simulated.
128 devices in a mesh: row: 8 (over z, core), col: 16 (over y, x).
Axes of the slice: x: 4, y: 4, z: 4, core: 2. Of those that a mesh axis runs over, the one named last changes fastest.
Arguments:
- inverse_interior: float32 [8, 16, 1536, 1536], P('row', 'col'), may hold values from -0.15625 to 0.15625
- coupling: float32 [8, 16, 1536, 1024], P('row', 'col'), may hold values from -1 to 1
- interface_block: float32 [8, 16, 1024, 1024], P('row', 'col'), may hold values from -6 to 6
- iface_ids: int32 [8, 16, 4], P('row', 'col'), may hold values from 0 to 15, as said below
- row_place: int32 [16], replicated, may hold values from 0 to 15, as said below
- col_place: int32 [16], replicated, may hold values from 0 to 15, as said below
Outputs:
- assembled: float32 [16, 256, 16, 256], P('row', None, 'col')
Inputs may be any that keep to these rules, and one draw needn't show every extreme that they name: `row_place`: A permutation of the tile ids. `col_place`: a permutation of the tile ids; two ids whose values of row_place differ mod 8 have values of col_place that differ mod 16. `iface_ids`: the 4 ids of one subdomain have pairwise different row_place mod 8, hence pairwise different col_place mod 16.
All inputs are finite; a program needn't handle non-finite values.
Results may differ from a plain program's by a relative error of at most 0.0001.
Values sent between devices are 32-bit elements; how exact they have to be, the bound alone decides.
No kernel may reach another device: no remote copies, remote signals or barrier semaphores. Data moves between devices by JAX's collectives and lax.ppermute only.
A program may use at most 192 MiB of HBM per device.

v0:
```python
import jax
import jax.numpy as jnp
from jax import lax
from jax.experimental import pallas as pl
from jax.experimental.pallas import tpu as pltpu
from jax.sharding import PartitionSpec as P

TILE = 256
AXES = ("row", "col")
STEP = 16


def combine_kernel(ids_ref, row_ref, col_ref, *refs):
    parts, out_ref = refs[:-1], refs[-1]
    step = pl.program_id(0)

    @pl.when(step == 0)
    def _():
        out_ref[...] = jnp.zeros(out_ref.shape, jnp.float32)

    def absorb(k, carry):
        source = step * STEP + k
        row_base, col_base = [], []
        for a in range(4):
            g = ids_ref[source, a]
            rp = row_ref[g]
            row_base.append((rp & 7) * 32 + (rp >> 3))
            col_base.append(col_ref[g] * 2)
        places, values = [], []
        count = 0
        for part in parts:
            for t in range(part.shape[1]):
                place = row_base[count // 4] + col_base[count % 4]
                places.append(place)
                values.append(out_ref[place] + part[k, t])
                count += 1
        for place, value in zip(places, values):
            out_ref[place] = value
        return carry

    lax.fori_loop(0, STEP, absorb, 0, unroll=2)


def combine(ids, row_place, col_place, parts):
    smem = pl.BlockSpec(memory_space=pltpu.SMEM)
    return pl.pallas_call(
        combine_kernel,
        grid=(ids.shape[0] // STEP,),
        in_specs=[smem, smem, smem]
        + [pl.BlockSpec((STEP,) + p.shape[1:], lambda s: (s, 0, 0, 0)) for p in parts],
        out_specs=pl.BlockSpec((256, 4, 128), lambda s: (0, 0, 0)),
        out_shape=jax.ShapeDtypeStruct((256, 4, 128), jnp.float32),
        name="combine",
    )(ids, row_place, col_place, *parts)


def on_device(inverse_interior, coupling, interface_block, iface_ids, row_place, col_place):
    inverse = inverse_interior[0, 0]
    couple = coupling[0, 0]
    block = interface_block[0, 0]
    ids = lax.all_to_all(
        jnp.broadcast_to(iface_ids[0, 0][None, :], (128, 4)), AXES, 0, 0, tiled=True
    )
    arrived = []
    for first, last in ((0, 2), (2, 4)):
        rows = slice(first * TILE, last * TILE)
        left = lax.dot_general(
            couple[:, rows],
            inverse,
            (((0,), (0,)), ((), ())),
            precision=lax.Precision.HIGH,
            preferred_element_type=jnp.float32,
        )
        schur = block[rows] - jnp.dot(
            left, couple, precision=lax.Precision.HIGH, preferred_element_type=jnp.float32
        )
        pieces = schur.reshape(last - first, 32, 2, 4, 4, 2, 128)
        pieces = pieces.transpose(1, 5, 2, 0, 4, 3, 6).reshape(128, (last - first) * 4, 4, 128)
        arrived.append(lax.all_to_all(pieces, AXES, 0, 0, tiled=True))
    total = combine(ids, row_place, col_place, arrived)
    owned = lax.all_to_all(total.reshape(128, 2, 4, 128), AXES, 0, 0, tiled=True)
    owned = owned.reshape(32, 2, 2, 2, 4, 128).transpose(3, 0, 2, 4, 1, 5)
    return owned.reshape(2, TILE, 1, TILE)


def solution(mesh):
    return jax.shard_map(
        on_device,
        mesh=mesh,
        in_specs=(
            P("row", "col", None, None),
            P("row", "col", None, None),
            P("row", "col", None, None),
            P("row", "col", None),
            P(),
            P(),
        ),
        out_specs=P("row", None, "col", None),
        check_vma=False,
    )
```

profile of v0, /device:TPU:1, one launch (start us, length us, event | category | flops | bytes accessed | tf_op | source)
XLA Modules:
  0.0 140.6 jit_solution(4589041508462861874)
XLA Ops:
  0.0 0.0 slice-start
  0.0 1.5 %broadcast_in_dim.2 = s32[128,1,4]{2,1,0:T(1,128)} broadcast(s32[4]{0:T(128)} %bitcast.40), dimensions={2} | broadcast | bytes 2064 | tf_op jit(solution)/shard_map/broadcast_in_dim | solution.py:62
  1.5 11.5 %all-to-all-start = ((s32[128,1,4]{2,1,0:T(1,128)}), s32[128,1,4]{2,1,0:T(1,128)S(1)}, u32[]{:S(2)}, u32[]{:S(2)}) async-start(s32[128,1,4]{2,1,0:T(1,128)} %broadcast_in_dim.2), calls=%async_computation | async-start | bytes 131072 | tf_op jit(solution)/shard_map/all_to_all | solution.py:61
  13.0 0.0 slice-start.1
  13.0 0.0 copy-start
  13.0 12.4 %fusion.2 = f32[512,1536]{1,0:T(8,128)S(1)} fusion(f32[1,1,1536,1536]{3,2,1,0:T(8,128)} %param.6, f32[1536,1024]{1,0:T(8,128)} %bitcast.29), kind=kOutput, calls=%fused_computation.2 | convolution fusion | flops 7247757312 | bytes 15728640 | tf_op jit(solution)/shard_map/dot_general | solution.py:67
  25.4 0.0 slice-done
  25.4 0.0 slice-done.1
  25.4 0.0 copy-done
  25.5 6.7 %bitcast_subtract_fusion.1 = f32[512,1024]{1,0:T(8,128)} fusion(f32[1,1,1024,1024]{3,2,1,0:T(8,128)S(1)} %copy-done, f32[512,1536]{1,0:T(8,128)S(1)} %fusion.2, f32[1,1,1536,1024]{3,2,1,0:T(8,128)S(1)} %bitcast.32), kind=kOutput, calls=%fused_computation.7 | convolution fusion | flops 4832362496 | bytes 13631488 | tf_op jit(solution)/shard_map/dot_general | solution.py:74
  32.1 3.0 %reshape.30 = f32[2,32,2,4,4,2,128]{6,5,4,3,2,1,0:T(2,128)S(1)} reshape(f32[512,1024]{1,0:T(8,128)} %bitcast_subtract_fusion.1) | data formatting | bytes 4194304 | tf_op jit(solution)/shard_map/reshape | solution.py:77
  35.2 1.9 %copy.10 = f32[2,32,2,4,4,2,128]{6,3,4,0,2,5,1:T(4,128)} copy(f32[2,32,2,4,4,2,128]{6,5,4,3,2,1,0:T(2,128)S(1)} %reshape.30) | data formatting | bytes 4194304 | tf_op jit(solution)/shard_map/reshape | solution.py:77
  37.1 0.0 all-to-all-done
  37.1 0.0 copy-start.2
  37.1 0.0 slice-start.2
  37.1 10.2 %all-to-all-start.1 = ((f32[128,8,4,128]{3,2,1,0:T(4,128)}), f32[128,8,4,128]{3,2,1,0:T(4,128)}, u32[]{:S(2)}, u32[]{:S(2)}) async-start(f32[128,8,4,128]{3,2,1,0:T(4,128)} %bitcast.35), calls=%async_computation.1 | async-start | bytes 4194304 | tf_op jit(solution)/shard_map/all_to_all | solution.py:79
  47.3 0.0 slice-start.3
  47.3 0.0 copy-start.1
  47.3 12.4 %fusion = f32[512,1536]{1,0:T(8,128)S(1)} fusion(f32[1,1,1536,1536]{3,2,1,0:T(8,128)} %param.6, f32[1536,1024]{1,0:T(8,128)} %bitcast.30), kind=kOutput, calls=%fused_computation | convolution fusion | flops 7247757312 | bytes 15728640 | tf_op jit(solution)/shard_map/dot_general | solution.py:67
  59.8 0.0 copy-done.2
  59.8 0.0 slice-done.2
  59.8 0.0 slice-done.3
  59.8 0.0 copy-done.1
  59.8 6.7 %bitcast_subtract_fusion = f32[512,1024]{1,0:T(8,128)} fusion(f32[1,1,1024,1024]{3,2,1,0:T(8,128)S(1)} %copy-done.1, f32[512,1536]{1,0:T(8,128)S(1)} %fusion, f32[1,1,1536,1024]{3,2,1,0:T(8,128)S(1)} %bitcast.34), kind=kOutput, calls=%fused_computation.6 | convolution fusion | flops 4832362496 | bytes 13631488 | tf_op jit(solution)/shard_map/dot_general | solution.py:74
  66.5 4.0 %reshape.32 = f32[2,32,2,4,4,2,128]{6,5,4,3,2,1,0:T(2,128)} reshape(f32[512,1024]{1,0:T(8,128)} %bitcast_subtract_fusion) | data formatting | bytes 4194304 | tf_op jit(solution)/shard_map/reshape | solution.py:77
  70.5 2.1 %copy.11 = f32[2,32,2,4,4,2,128]{6,3,4,0,2,5,1:T(4,128)S(1)} copy(f32[2,32,2,4,4,2,128]{6,5,4,3,2,1,0:T(2,128)} %reshape.32) | data formatting | bytes 4194304 | tf_op jit(solution)/shard_map/reshape | solution.py:77
  72.7 4.0 %all-to-all-done.1.refs_0_ = f32[128,8,4,128]{3,2,1,0:T(4,128)} async-done(((f32[128,8,4,128]{3,2,1,0:T(4,128)}), f32[128,8,4,128]{3,2,1,0:T(4,128)}, u32[]{:S(2)}, u32[]{:S(2)}) %all-to-all-start.1) | async-done | bytes 2097184 | tf_op jit(solution)/shard_map/all_to_all | solution.py:79
  76.6 35.4 %all_to_all.23.refs_1_ = f32[128,8,4,128]{3,2,1,0:T(4,128)} all-to-all(f32[128,8,4,128]{3,2,1,0:T(4,128)S(1)} %bitcast.36), channel_id=1, replica_groups=mesh['row'=8,'col'=16] {'row','col'}, dimensions={0} | all-to-all | bytes 4194304 | tf_op jit(solution)/shard_map/all_to_all | solution.py:79
  112.1 8.7 %combine.1 = f32[256,4,128]{2,1,0:T(4,128)} custom-call(s32[128,4]{1,0:T(8,128)} %bitcast.39, s32[16]{0:T(128)} %row_ref.1, s32[16]{0:T(128)} %col_ref.1, f32[128,8,4,128]{3,2,1,0:T(4,128)} %all-to-all-done.1.refs_0_, f32[128,8,4,128]{3,2,1,0:T(4,128)} %all_to_all.23.refs_1_), custom_call_target="tpu_custom_call" | custom-call | tf_op jit(solution)/shard_map/combine/pallas_call | solution.py:46
  120.7 18.8 %all_to_all.24 = f32[128,2,4,128]{3,2,1,0:T(4,128)S(1)} all-to-all(f32[128,2,4,128]{3,2,1,0:T(4,128)} %bitcast.38), channel_id=1, replica_groups=mesh['row'=8,'col'=16] {'row','col'}, dimensions={0} | all-to-all | bytes 1048576 | tf_op jit(solution)/shard_map/all_to_all | solution.py:81
  139.6 1.1 copy.12
  (2 shorter events, 0.0 us)
Async XLA Ops:
  0.0 25.4 %slice-start = ((s8[6291456]{0:T(1024)(128)(4,1)}), s8[2097152]{0:T(1024)(128)(4,1)S(1)}, s32[]{:S(2)}) async-start(s8[6291456]{0:T(1024)(128)(4,1)} %bitcast.31), calls=%async_computation.4 | async-start | bytes 4194304
  1.5 35.6 %all-to-all-start = ((s32[128,1,4]{2,1,0:T(1,128)}), s32[128,1,4]{2,1,0:T(1,128)S(1)}, u32[]{:S(2)}, u32[]{:S(2)}) async-start(s32[128,1,4]{2,1,0:T(1,128)} %broadcast_in_dim.2), calls=%async_computation | async-start | bytes 131072 | tf_op jit(solution)/shard_map/all_to_all | solution.py:61
  13.0 12.5 %slice-start.1 = ((s8[6291456]{0:T(1024)(128)(4,1)}), s8[4194304]{0:T(1024)(128)(4,1)S(1)}, s32[]{:S(2)}) async-start(s8[6291456]{0:T(1024)(128)(4,1)} %bitcast.31), calls=%async_computation.5 | async-start | bytes 8388608
  13.0 12.5 %copy-start = (f32[1,1,1024,1024]{3,2,1,0:T(8,128)S(1)}, f32[1,1,1024,1024]{3,2,1,0:T(8,128)}, u32[]{:S(2)}) copy-start(f32[1,1,1024,1024]{3,2,1,0:T(8,128)} %param.8) | copy-start | bytes 12582916
  37.1 22.7 %copy-start.2 = (s32[128,1,4]{2,1,0:T(1,128)}, s32[128,1,4]{2,1,0:T(1,128)S(1)}, u32[]{:S(2)}) copy-start(s32[128,1,4]{2,1,0:T(1,128)S(1)} %all-to-all-done) | copy-start | bytes 6148
  37.1 22.7 %slice-start.2 = ((s8[6291456]{0:T(1024)(128)(4,1)}), s8[2097152]{0:T(1024)(128)(4,1)S(1)}, s32[]{:S(2)}) async-start(s8[6291456]{0:T(1024)(128)(4,1)} %bitcast.33), calls=%async_computation.6 | async-start | bytes 4194304
  37.1 39.6 %all-to-all-start.1 = ((f32[128,8,4,128]{3,2,1,0:T(4,128)}), f32[128,8,4,128]{3,2,1,0:T(4,128)}, u32[]{:S(2)}, u32[]{:S(2)}) async-start(f32[128,8,4,128]{3,2,1,0:T(4,128)} %bitcast.35), calls=%async_computation.1 | async-start | bytes 4194304 | tf_op jit(solution)/shard_map/all_to_all | solution.py:79
  47.3 12.5 %slice-start.3 = ((s8[6291456]{0:T(1024)(128)(4,1)}), s8[4194304]{0:T(1024)(128)(4,1)S(1)}, s32[]{:S(2)}) async-start(s8[6291456]{0:T(1024)(128)(4,1)} %bitcast.33), calls=%async_computation.7 | async-start | bytes 8388608
  47.3 12.5 %copy-start.1 = (f32[1,1,1024,1024]{3,2,1,0:T(8,128)S(1)}, f32[1,1,1024,1024]{3,2,1,0:T(8,128)}, u32[]{:S(2)}) copy-start(f32[1,1,1024,1024]{3,2,1,0:T(8,128)} %param.8) | copy-start | bytes 12582916
where the time goes:
time: 141 us
  blocking collectives  54.2 us (38%)
  matrix products  38.2 us (27%)
  starting transfers between devices  21.7 us (15%)
  local copies, waits for them, and re-layouts  13.7 us (10%)
  Pallas kernels  8.66 us (6%)
  waiting for transfers between devices  3.95 us (3%)
    all_to_all x1, blocking collectives, on_device(): arrived.append(lax.all_to_all(pieces, AXES, 0, 0, tiled=True))  35.4 us
    dot_general x2, matrix products, on_device(): lax.dot_general(couple[:, rows], inverse, (((0,), (0,)), ((), ())), preci...  24.9 us
    all_to_all x1, blocking collectives, on_device(): lax.all_to_all(total.reshape(128, 2, 4, 128), AXES, 0, 0, tiled=True)  18.8 us
    dot_general x2, matrix products, on_device(): jnp.dot(left, couple, precision=lax.Precision.HIGH, preferred_element_typ...  13.4 us
    all_to_all x1, starting transfers between devices, on_device(): lax.all_to_all(jnp.broadcast_to(iface_ids[0, 0][None, :], (128, 4)), AXES...  11.5 us
    reshape x4, local copies, waits for them, and re-layouts, on_device(): pieces = schur.reshape(last - first, 32, 2, 4, 4, 2, 128)  11.1 us
    all_to_all x1, starting transfers between devices, on_device(): arrived.append(lax.all_to_all(pieces, AXES, 0, 0, tiled=True))  10.2 us
    pallas_call x1, Pallas kernels, combine(): pl.pallas_call(combine_kernel, grid=(ids.shape[0] // STEP,), in_specs=[sm...  8.66 us
  transfers between devices with their start and end apart: 2, of which 1 were waited for; matrix products, arithmetic and copies ran while one was open for 35% of the time, Pallas kernels for 0%

commit v1 on v0

v1 whole, which is shorter than its diff:
```python
import functools

import jax
import jax.numpy as jnp
from jax import lax
from jax.experimental import pallas as pl
from jax.experimental.pallas import tpu as pltpu
from jax.sharding import PartitionSpec as P

TILE = 256
AXES = ("row", "col")
SOLVE_ROWS = 512
SCHUR_ROWS = 512
PACK = 65


def split(x):
    high = x.astype(jnp.bfloat16)
    return high, (x - high.astype(jnp.float32)).astype(jnp.bfloat16)


def dot3(xh, xl, yh, yl, dims):
    def dot(x, y):
        return lax.dot_general(x, y, (dims, ((), ())), preferred_element_type=jnp.float32)

    return dot(xh, yh) + (dot(xh, yl) + dot(xl, yh))


def schur_kernel(
    ids_ref, row_ref, col_ref, inverse_ref, couple_ref, block_ref, out_ref, ch_ref, cl_ref, uh_ref, ul_ref, *, solves, schurs
):
    step = pl.program_id(0)

    @pl.when(step == 0)
    def _():
        ch_ref[...], cl_ref[...] = split(couple_ref[...])
        lane = lax.broadcasted_iota(jnp.int32, (128, 128), 1)
        marks = jnp.zeros((128, 128), jnp.int32)
        for t in range(16):
            row = row_ref[ids_ref[t // 4]]
            col = col_ref[ids_ref[t % 4]]
            place = ((row & 7) * 16 + col) * 2 + (row >> 3)
            marks = jnp.where(lane == t, place, marks)
        out_ref[pl.ds(64, 128, stride=PACK), :] = marks.astype(jnp.float32)

    @pl.when(step < solves)
    def _():
        high, low = split(inverse_ref[...])
        solved = dot3(high, low, ch_ref[...], cl_ref[...], ((1,), (0,)))
        rows = pl.ds(step * SOLVE_ROWS, SOLVE_ROWS)
        uh_ref[rows, :], ul_ref[rows, :] = split(solved)

    for part in range(schurs):

        @pl.when(step == solves + part)
        def _():
            cols = slice(part * SCHUR_ROWS, (part + 1) * SCHUR_ROWS)
            product = dot3(ch_ref[:, cols], cl_ref[:, cols], uh_ref[...], ul_ref[...], ((0,), (0,)))
            schur = block_ref[...] - product
            for t in range(SCHUR_ROWS // TILE * 4):
                a, b = divmod(t, 4)
                for lane in range(2):
                    left = b * TILE + lane * 128
                    for group in range(32):
                        for half in range(2):
                            top = a * TILE + group * 8 + half * 4
                            start = (group * 4 + lane * 2 + half) * PACK + (part * SCHUR_ROWS // TILE * 4 + t) * 4
                            out_ref[start : start + 4, :] = schur[top : top + 4, left : left + 128]


def schur_tiles(ids, row_place, col_place, inverse, couple, block):
    inner, outer = couple.shape
    solves, schurs = inner // SOLVE_ROWS, outer // SCHUR_ROWS
    smem = pl.BlockSpec(memory_space=pltpu.SMEM)
    return pl.pallas_call(
        functools.partial(schur_kernel, solves=solves, schurs=schurs),
        grid=(solves + schurs,),
        in_specs=[
            smem,
            smem,
            smem,
            pl.BlockSpec((SOLVE_ROWS, inner), lambda s: (jnp.minimum(s, solves - 1), 0)),
            pl.BlockSpec((inner, outer), lambda s: (0, 0)),
            pl.BlockSpec((SCHUR_ROWS, outer), lambda s: (jnp.clip(s - solves, 0, schurs - 1), 0)),
        ],
        out_specs=pl.BlockSpec(memory_space=pltpu.VMEM),
        out_shape=pltpu.VMEM((128 * PACK, 128), jnp.float32),
        scratch_shapes=[pltpu.VMEM((inner, outer), jnp.bfloat16)] * 4,
        compiler_params=pltpu.CompilerParams(vmem_limit_bytes=54 * 1024 * 1024),
        cost_estimate=pl.CostEstimate(flops=24 * 10**9, bytes_accessed=25 * 10**6, transcendentals=0),
        name="schur",
    )(ids, row_place, col_place, inverse, couple, block)


def combine_kernel(part_ref, out_ref, place_ref, high_ref, low_ref):
    marks = part_ref[pl.ds(64, 128, stride=PACK), :]
    spots = lax.broadcasted_iota(jnp.int32, (128, 256), 1).astype(jnp.float32)
    for t in range(16):
        rows = slice(t * 128, (t + 1) * 128)
        hit = jnp.broadcast_to(marks[:, t : t + 1], (128, 256)) == spots
        place_ref[rows, :] = jnp.where(hit, 1.0, 0.0).astype(jnp.bfloat16)
        for r in range(4):
            lanes = slice(r * 128, (r + 1) * 128)
            values = part_ref[pl.ds(t * 4 + r, 128, stride=PACK), :]
            high_ref[rows, lanes], low_ref[rows, lanes] = split(values)

    def total(values):
        return lax.dot_general(
            place_ref[...], values, (((0,), (0,)), ((), ())), preferred_element_type=jnp.float32
        )

    sums = total(high_ref[...]) + total(low_ref[...])
    for r in range(4):
        out_ref[pl.ds(r, 256, stride=4), :] = sums[:, r * 128 : (r + 1) * 128]


def combine(parts):
    parts = pltpu.with_memory_space_constraint(parts, pltpu.VMEM)
    return pl.pallas_call(
        combine_kernel,
        in_specs=[pl.BlockSpec(memory_space=pltpu.VMEM)],
        out_specs=pl.BlockSpec(memory_space=pltpu.VMEM),
        out_shape=pltpu.VMEM((1024, 128), jnp.float32),
        scratch_shapes=[
            pltpu.VMEM((2048, 256), jnp.bfloat16),
            pltpu.VMEM((2048, 512), jnp.bfloat16),
            pltpu.VMEM((2048, 512), jnp.bfloat16),
        ],
        compiler_params=pltpu.CompilerParams(vmem_limit_bytes=24 * 1024 * 1024),
        name="combine",
    )(parts)


def on_device(inverse_interior, coupling, interface_block, iface_ids, row_place, col_place):
    pieces = schur_tiles(
        iface_ids[0, 0], row_place, col_place, inverse_interior[0, 0], coupling[0, 0], interface_block[0, 0]
    )
    arrived = lax.all_to_all(pieces.reshape(128, PACK, 1, 128), AXES, 0, 0, tiled=True)
    total = combine(arrived.reshape(128 * PACK, 128))
    owned = lax.all_to_all(total.reshape(128, 8, 128), AXES, 0, 0, tiled=True)
    owned = owned.reshape(32, 2, 2, 2, 4, 128).transpose(3, 0, 2, 4, 1, 5)
    return owned.reshape(2, TILE, 1, TILE)


def solution(mesh):
    return jax.shard_map(
        on_device,
        mesh=mesh,
        in_specs=(
            P("row", "col", None, None),
            P("row", "col", None, None),
            P("row", "col", None, None),
            P("row", "col", None),
            P(),
            P(),
        ),
        out_specs=P("row", None, "col", None),
        check_vma=False,
    )
```

time: 141 us -> 118 us (0.84)
  matrix products: 38.2 us -> 0 us
  blocking collectives: 54.2 us -> 83.4 us
  Pallas kernels: 8.66 us -> 33.1 us
  starting transfers between devices: 21.7 us -> 0 us
  local copies, waits for them, and re-layouts: 13.7 us -> 1.06 us
  waiting for transfers between devices: 3.95 us -> 0 us
    dot_general x4 -> x0, matrix products: 38.2 us -> none  [the longest x2 24.9 us: on_device(): lax.dot_general(couple[:, rows], inverse, (((0,), (0,)), ((), ())), preci...]
    all_to_all x2, blocking collectives: 54.2 us -> 83.4 us  [the longest x1 65.3 us: on_device(): lax.all_to_all(pieces.reshape(128, PACK, 1, 128), AXES, 0, 0, tiled=True)]
    pallas_call x1 -> x2, Pallas kernels: 8.66 us -> 33.1 us  [the longest x1 31 us: schur_tiles(): pl.pallas_call(functools.partial(schur_kernel, solves=solves, schurs=schu...]
    all_to_all x2 -> x0, starting transfers between devices: 21.7 us -> none  [the longest x1 11.5 us: on_device(): lax.all_to_all(jnp.broadcast_to(iface_ids[0, 0][None, :], (128, 4)), AXES...]
    reshape x4 -> x0, local copies, waits for them, and re-layouts: 11.1 us -> none  [on_device(): pieces = schur.reshape(last - first, 32, 2, 4, 4, 2, 128)]
    all_to_all x2 -> x0, waiting for transfers between devices: 3.95 us -> none  [the longest x1 3.95 us: on_device(): arrived.append(lax.all_to_all(pieces, AXES, 0, 0, tiled=True))]
    broadcast_in_dim x1 -> x0, local copies, waits for them, and re-layouts: 1.47 us -> none  [on_device(): jnp.broadcast_to(iface_ids[0, 0][None, :], (128, 4))]
  transfers between devices with their start and end apart: 2 -> 0, of which waited for: 1 -> 0; matrix products, arithmetic and copies ran while one was open for 35% -> 0% of each run, Pallas kernels for 0% -> 0%
where the time goes in v1:
time: 118 us
  blocking collectives  83.4 us (71%)
  Pallas kernels  33.1 us (28%)
    all_to_all x1, blocking collectives, on_device(): lax.all_to_all(pieces.reshape(128, PACK, 1, 128), AXES, 0, 0, tiled=True)  65.3 us
    pallas_call x1, Pallas kernels, schur_tiles(): pl.pallas_call(functools.partial(schur_kernel, solves=solves, schurs=schu...  31 us
    all_to_all x1, blocking collectives, on_device(): owned = lax.all_to_all(total.reshape(128, 8, 128), AXES, 0, 0, tiled=True)  18.1 us

profile of v1, /device:TPU:1, one launch (start us, length us, event | category | flops | bytes accessed | tf_op | source)
XLA Modules:
  0.0 117.6 jit_solution(7669802738197773513)
XLA Ops:
  0.0 31.0 %schur.1 = f32[8320,128]{1,0:T(8,128)S(1)} custom-call(s32[4]{0:T(128)} %bitcast.18, s32[16]{0:T(128)} %row_ref.1, s32[16]{0:T(128)} %col_ref.1, f32[1536,1536]{1,0:T(8,128)} %bitcast.15, f32[1536,1024]{1,0:T(8,128)} %bitcast.16, f32[1024,1024]{1,0:T(8,128)} %bitcast.17), custom_call_target="tpu_custom_call" | custom-call | flops 24000000000 | bytes 25000000 | tf_op jit(solution)/shard_map/schur/pallas_call | solution.py:75
  31.0 65.3 %all_to_all.10 = f32[128,65,1,128]{3,2,1,0:T(1,128)S(1)} all-to-all(f32[128,65,1,128]{3,2,1,0:T(1,128)S(1)} %bitcast.12), channel_id=1, replica_groups=mesh['row'=8,'col'=16] {'row','col'}, dimensions={0} | all-to-all | bytes 8519680 | tf_op jit(solution)/shard_map/all_to_all | solution.py:138
  96.3 2.1 %combine.1 = f32[1024,128]{1,0:T(8,128)S(1)} custom-call(f32[8320,128]{1,0:T(8,128)S(1)} %bitcast.11), custom_call_target="tpu_custom_call" | custom-call | tf_op jit(solution)/shard_map/combine/pallas_call | solution.py:119
  98.4 18.1 %all_to_all.11 = f32[128,8,128]{2,1,0:T(8,128)S(1)} all-to-all(f32[128,8,128]{2,1,0:T(8,128)S(1)} %bitcast.13), channel_id=1, replica_groups=mesh['row'=8,'col'=16] {'row','col'}, dimensions={0} | all-to-all | bytes 1048576 | tf_op jit(solution)/shard_map/all_to_all | solution.py:140
  116.5 1.1 copy.10

commit v2 on v1

v2 whole, which is shorter than its diff:
```python
import functools

import jax
import jax.numpy as jnp
from jax import lax
from jax.experimental import pallas as pl
from jax.experimental.pallas import tpu as pltpu
from jax.sharding import PartitionSpec as P

TILE = 256
AXES = ("row", "col")
DEPTH = 256
SCHUR_ROWS = 512
PACK = 65


def pack_row(a, u, b, h):
    return a * 16 + u * 8 + b * 2 + h


def split(x):
    high = x.astype(jnp.bfloat16)
    return high, (x - high.astype(jnp.float32)).astype(jnp.bfloat16)


def dot(x, y, dims):
    return lax.dot_general(x, y, (dims, ((), ())), preferred_element_type=jnp.float32)


def schur_kernel(
    ids_ref,
    row_ref,
    col_ref,
    inverse_ref,
    couple_ref,
    block_hbm,
    out_ref,
    left_ref,
    right_ref,
    ch_ref,
    cl_ref,
    sum_ref,
    uh_ref,
    ul_ref,
    block_ref,
    block_sem,
    *,
    depths,
    schurs,
):
    step = pl.program_id(0)
    fetch = pltpu.make_async_copy(block_hbm, block_ref, block_sem)

    @pl.when(step == 0)
    def _():
        lane = lax.broadcasted_iota(jnp.int32, (128, 128), 1)
        marks = jnp.zeros((128, 128), jnp.int32)
        for t in range(16):
            row = row_ref[ids_ref[t // 4]]
            col = col_ref[ids_ref[t % 4]]
            place = ((row & 7) * 16 + col) * 2 + (row >> 3)
            marks = jnp.where(lane == t, place, marks)
        out_ref[pl.ds(64, 128, stride=PACK), :] = marks.astype(jnp.float32)

    def partial():
        high, low = split(inverse_ref[...])
        left_ref[:, :DEPTH] = high
        left_ref[:, DEPTH : 2 * DEPTH] = low
        left_ref[:, 2 * DEPTH :] = high
        high, low = split(couple_ref[...])
        right_ref[:DEPTH, :] = high
        right_ref[DEPTH : 2 * DEPTH, :] = high
        right_ref[2 * DEPTH :, :] = low
        rows = pl.ds(step * DEPTH, DEPTH)
        ch_ref[rows, :] = high
        cl_ref[rows, :] = low
        return dot(left_ref[...], right_ref[...], ((1,), (0,)))

    @pl.when(step == 0)
    def _():
        sum_ref[...] = partial()

    @pl.when((step > 0) & (step < depths - 1))
    def _():
        sum_ref[...] += partial()

    @pl.when(step == 1)
    def _():
        fetch.start()

    @pl.when(step == depths - 1)
    def _():
        uh_ref[...], ul_ref[...] = split(sum_ref[...] + partial())
        fetch.wait()

    for part in range(schurs):

        @pl.when(step == depths + part)
        def _():
            cols = slice(part * SCHUR_ROWS, (part + 1) * SCHUR_ROWS)
            ch, cl, uh, ul = ch_ref[:, cols], cl_ref[:, cols], uh_ref[...], ul_ref[...]
            across = ((0,), (0,))
            schur = block_ref[cols, :] - (dot(ch, uh, across) + (dot(ch, ul, across) + dot(cl, uh, across)))
            for n in range(SCHUR_ROWS // 128):
                a, u = divmod(part * SCHUR_ROWS // 128 + n, 2)
                for b in range(4):
                    for h in range(2):
                        left = b * TILE + h * 128
                        out_ref[pl.ds(pack_row(a, u, b, h), 128, stride=PACK), :] = schur[
                            n * 128 : (n + 1) * 128, left : left + 128
                        ]


def schur_tiles(ids, row_place, col_place, inverse, couple, block):
    inner, outer = couple.shape
    depths, schurs = inner // DEPTH, outer // SCHUR_ROWS
    smem = pl.BlockSpec(memory_space=pltpu.SMEM)
    return pl.pallas_call(
        functools.partial(schur_kernel, depths=depths, schurs=schurs),
        grid=(depths + schurs,),
        in_specs=[
            smem,
            smem,
            smem,
            pl.BlockSpec((inner, DEPTH), lambda s: (0, jnp.minimum(s, depths - 1))),
            pl.BlockSpec((DEPTH, outer), lambda s: (jnp.minimum(s, depths - 1), 0)),
            pl.BlockSpec(memory_space=pltpu.HBM),
        ],
        out_specs=pl.BlockSpec(memory_space=pltpu.VMEM),
        out_shape=pltpu.VMEM((128 * PACK, 128), jnp.float32),
        scratch_shapes=[
            pltpu.VMEM((inner, 3 * DEPTH), jnp.bfloat16),
            pltpu.VMEM((3 * DEPTH, outer), jnp.bfloat16),
            pltpu.VMEM((inner, outer), jnp.bfloat16),
            pltpu.VMEM((inner, outer), jnp.bfloat16),
            pltpu.VMEM((inner, outer), jnp.float32),
            pltpu.VMEM((inner, outer), jnp.bfloat16),
            pltpu.VMEM((inner, outer), jnp.bfloat16),
            pltpu.VMEM((outer, outer), jnp.float32),
            pltpu.SemaphoreType.DMA,
        ],
        compiler_params=pltpu.CompilerParams(vmem_limit_bytes=56 * 1024 * 1024),
        cost_estimate=pl.CostEstimate(flops=24 * 10**9, bytes_accessed=25 * 10**6, transcendentals=0),
        name="schur",
    )(ids, row_place, col_place, inverse, couple, block)


def combine_kernel(part_ref, out_ref, place_ref, high_ref, low_ref):
    marks = part_ref[pl.ds(64, 128, stride=PACK), :]
    spots = lax.broadcasted_iota(jnp.int32, (128, 256), 1).astype(jnp.float32)
    for t in range(16):
        rows = slice(t * 128, (t + 1) * 128)
        hit = jnp.broadcast_to(marks[:, t : t + 1], (128, 256)) == spots
        place_ref[rows, :] = jnp.where(hit, 1.0, 0.0).astype(jnp.bfloat16)
        for r in range(4):
            lanes = slice(r * 128, (r + 1) * 128)
            row = pack_row(t // 4, r // 2, t % 4, r % 2)
            values = part_ref[pl.ds(row, 128, stride=PACK), :]
            high_ref[rows, lanes], low_ref[rows, lanes] = split(values)

    def total(values):
        return lax.dot_general(
            place_ref[...], values, (((0,), (0,)), ((), ())), preferred_element_type=jnp.float32
        )

    sums = total(high_ref[...]) + total(low_ref[...])
    for r in range(4):
        out_ref[pl.ds(r, 256, stride=4), :] = sums[:, r * 128 : (r + 1) * 128]


def combine(parts):
    parts = pltpu.with_memory_space_constraint(parts, pltpu.VMEM)
    return pl.pallas_call(
        combine_kernel,
        in_specs=[pl.BlockSpec(memory_space=pltpu.VMEM)],
        out_specs=pl.BlockSpec(memory_space=pltpu.VMEM),
        out_shape=pltpu.VMEM((1024, 128), jnp.float32),
        scratch_shapes=[
            pltpu.VMEM((2048, 256), jnp.bfloat16),
            pltpu.VMEM((2048, 512), jnp.bfloat16),
            pltpu.VMEM((2048, 512), jnp.bfloat16),
        ],
        compiler_params=pltpu.CompilerParams(vmem_limit_bytes=24 * 1024 * 1024),
        name="combine",
    )(parts)


def on_device(inverse_interior, coupling, interface_block, iface_ids, row_place, col_place):
    pieces = schur_tiles(
        iface_ids[0, 0], row_place, col_place, inverse_interior[0, 0], coupling[0, 0], interface_block[0, 0]
    )
    arrived = lax.all_to_all(pieces.reshape(128, PACK, 1, 128), AXES, 0, 0, tiled=True)
    total = combine(arrived.reshape(128 * PACK, 128))
    owned = lax.all_to_all(total.reshape(128, 8, 128), AXES, 0, 0, tiled=True)
    owned = owned.reshape(128, 2, 2, 2, 128).transpose(1, 2, 0, 3, 4)
    return owned.reshape(2, TILE, 1, TILE)


def solution(mesh):
    return jax.shard_map(
        on_device,
        mesh=mesh,
        in_specs=(
            P("row", "col", None, None),
            P("row", "col", None, None),
            P("row", "col", None, None),
            P("row", "col", None),
            P(),
            P(),
        ),
        out_specs=P("row", None, "col", None),
        check_vma=False,
    )
```

time: 118 us -> 116 us (0.983)
  Pallas kernels: 33.1 us -> 31 us
    pallas_call x1, Pallas kernels: 31 us -> 28.9 us  [schur_tiles(): pl.pallas_call(functools.partial(schur_kernel, depths=depths, schurs=schu...]
where the time goes in v2:
time: 116 us; the launch traced here: 115 us
  blocking collectives  83.4 us (72%)
  Pallas kernels  31 us (27%)
    all_to_all x1, blocking collectives, on_device(): lax.all_to_all(pieces.reshape(128, PACK, 1, 128), AXES, 0, 0, tiled=True)  65.3 us
    pallas_call x1, Pallas kernels, schur_tiles(): pl.pallas_call(functools.partial(schur_kernel, depths=depths, schurs=schu...  28.9 us
    all_to_all x1, blocking collectives, on_device(): owned = lax.all_to_all(total.reshape(128, 8, 128), AXES, 0, 0, tiled=True)  18.1 us

profile of v2, /device:TPU:1, one launch (start us, length us, event | category | flops | bytes accessed | tf_op | source)
XLA Modules:
  0.0 115.4 jit_solution(4679401873927508966)
XLA Ops:
  0.0 28.9 %schur.1 = f32[8320,128]{1,0:T(8,128)S(1)} custom-call(s32[4]{0:T(128)} %bitcast.18, s32[16]{0:T(128)} %row_ref.1, s32[16]{0:T(128)} %col_ref.1, f32[1536,1536]{1,0:T(8,128)} %bitcast.15, f32[1536,1024]{1,0:T(8,128)} %bitcast.16, f32[1024,1024]{1,0:T(8,128)} %bitcast.17), custom_call_target="tpu_custom_call" | custom-call | flops 24000000000 | bytes 25000000 | tf_op jit(solution)/shard_map/schur/pallas_call | solution.py:118
  28.9 65.3 %all_to_all.10 = f32[128,65,1,128]{3,2,1,0:T(1,128)S(1)} all-to-all(f32[128,65,1,128]{3,2,1,0:T(1,128)S(1)} %bitcast.12), channel_id=1, replica_groups=mesh['row'=8,'col'=16] {'row','col'}, dimensions={0} | all-to-all | bytes 8519680 | tf_op jit(solution)/shard_map/all_to_all | solution.py:192
  94.2 2.1 %combine.1 = f32[1024,128]{1,0:T(8,128)S(1)} custom-call(f32[8320,128]{1,0:T(8,128)S(1)} %bitcast.11), custom_call_target="tpu_custom_call" | custom-call | tf_op jit(solution)/shard_map/combine/pallas_call | solution.py:173
  96.3 18.1 %all_to_all.11 = f32[128,8,128]{2,1,0:T(8,128)S(1)} all-to-all(f32[128,8,128]{2,1,0:T(8,128)S(1)} %bitcast.13), channel_id=1, replica_groups=mesh['row'=8,'col'=16] {'row','col'}, dimensions={0} | all-to-all | bytes 1048576 | tf_op jit(solution)/shard_map/all_to_all | solution.py:194
  114.4 1.0 copy.10

commit v3 on v2

--- a/solution.py
+++ b/solution.py
@@ -145,25 +145,24 @@
     )(ids, row_place, col_place, inverse, couple, block)
 
 
-def combine_kernel(part_ref, out_ref, place_ref, high_ref, low_ref):
-    marks = part_ref[pl.ds(64, 128, stride=PACK), :]
-    spots = lax.broadcasted_iota(jnp.int32, (128, 256), 1).astype(jnp.float32)
-    for t in range(16):
-        rows = slice(t * 128, (t + 1) * 128)
-        hit = jnp.broadcast_to(marks[:, t : t + 1], (128, 256)) == spots
-        place_ref[rows, :] = jnp.where(hit, 1.0, 0.0).astype(jnp.bfloat16)
-        for r in range(4):
-            lanes = slice(r * 128, (r + 1) * 128)
-            row = pack_row(t // 4, r // 2, t % 4, r % 2)
-            values = part_ref[pl.ds(row, 128, stride=PACK), :]
-            high_ref[rows, lanes], low_ref[rows, lanes] = split(values)
-
-    def total(values):
-        return lax.dot_general(
-            place_ref[...], values, (((0,), (0,)), ((), ())), preferred_element_type=jnp.float32
-        )
-
-    sums = total(high_ref[...]) + total(low_ref[...])
+def combine_kernel(part_ref, out_ref):
+    marks = part_ref[pl.ds(64, 128, stride=PACK), :].T
+    spots = lax.broadcasted_iota(jnp.int32, (256, 128), 0).astype(jnp.float32)
+    sums = jnp.zeros((256, 512), jnp.float32)
+    for a in range(4):
+        places, highs, lows = [], [], []
+        for b in range(4):
+            t = a * 4 + b
+            hit = jnp.broadcast_to(marks[t : t + 1, :], (256, 128)) == spots
+            places.append(jnp.where(hit, 1.0, 0.0).astype(jnp.bfloat16))
+            values = jnp.concatenate(
+                [part_ref[pl.ds(pack_row(a, r // 2, b, r % 2), 128, stride=PACK), :] for r in range(4)], axis=1
+            )
+            high, low = split(values)
+            highs.append(high)
+            lows.append(low)
+        place = jnp.concatenate(places + places, axis=1)
+        sums = sums + jnp.dot(place, jnp.concatenate(highs + lows, axis=0), preferred_element_type=jnp.float32)
     for r in range(4):
         out_ref[pl.ds(r, 256, stride=4), :] = sums[:, r * 128 : (r + 1) * 128]
 
@@ -175,11 +174,6 @@
         in_specs=[pl.BlockSpec(memory_space=pltpu.VMEM)],
         out_specs=pl.BlockSpec(memory_space=pltpu.VMEM),
         out_shape=pltpu.VMEM((1024, 128), jnp.float32),
-        scratch_shapes=[
-            pltpu.VMEM((2048, 256), jnp.bfloat16),
-            pltpu.VMEM((2048, 512), jnp.bfloat16),
-            pltpu.VMEM((2048, 512), jnp.bfloat16),
-        ],
         compiler_params=pltpu.CompilerParams(vmem_limit_bytes=24 * 1024 * 1024),
         name="combine",
     )(parts)

time: 116 us -> 115 us (level)
  no operation moved by 1% of the time
where the time goes in v3:
time: 115 us
  blocking collectives  83.4 us (73%)
  Pallas kernels  30.2 us (26%)
    all_to_all x1, blocking collectives, on_device(): lax.all_to_all(pieces.reshape(128, PACK, 1, 128), AXES, 0, 0, tiled=True)  65.3 us
    pallas_call x1, Pallas kernels, schur_tiles(): pl.pallas_call(functools.partial(schur_kernel, depths=depths, schurs=schu...  28.9 us
    all_to_all x1, blocking collectives, on_device(): owned = lax.all_to_all(total.reshape(128, 8, 128), AXES, 0, 0, tiled=True)  18.1 us

profile of v3, /device:TPU:1, one launch (start us, length us, event | category | flops | bytes accessed | tf_op | source)
XLA Modules:
  0.0 114.6 jit_solution(1196746759491114065)
XLA Ops:
  0.0 28.9 %schur.1 = f32[8320,128]{1,0:T(8,128)S(1)} custom-call(s32[4]{0:T(128)} %bitcast.18, s32[16]{0:T(128)} %row_ref.1, s32[16]{0:T(128)} %col_ref.1, f32[1536,1536]{1,0:T(8,128)} %bitcast.15, f32[1536,1024]{1,0:T(8,128)} %bitcast.16, f32[1024,1024]{1,0:T(8,128)} %bitcast.17), custom_call_target="tpu_custom_call" | custom-call | flops 24000000000 | bytes 25000000 | tf_op jit(solution)/shard_map/schur/pallas_call | solution.py:118
  28.9 65.3 %all_to_all.10 = f32[128,65,1,128]{3,2,1,0:T(1,128)S(1)} all-to-all(f32[128,65,1,128]{3,2,1,0:T(1,128)S(1)} %bitcast.12), channel_id=1, replica_groups=mesh['row'=8,'col'=16] {'row','col'}, dimensions={0} | all-to-all | bytes 8519680 | tf_op jit(solution)/shard_map/all_to_all | solution.py:186
  94.2 1.3 %combine.1 = f32[1024,128]{1,0:T(8,128)S(1)} custom-call(f32[8320,128]{1,0:T(8,128)S(1)} %bitcast.11), custom_call_target="tpu_custom_call" | custom-call | tf_op jit(solution)/shard_map/combine/pallas_call | solution.py:172
  95.5 18.1 %all_to_all.11 = f32[128,8,128]{2,1,0:T(8,128)S(1)} all-to-all(f32[128,8,128]{2,1,0:T(8,128)S(1)} %bitcast.13), channel_id=1, replica_groups=mesh['row'=8,'col'=16] {'row','col'}, dimensions={0} | all-to-all | bytes 1048576 | tf_op jit(solution)/shard_map/all_to_all | solution.py:188
  113.6 1.0 copy.10

commit v4 on v3

--- a/solution.py
+++ b/solution.py
@@ -9,8 +9,8 @@
 
 TILE = 256
 AXES = ("row", "col")
-DEPTH = 256
-SCHUR_ROWS = 512
+CUTS = (0, 256, 768, 1536)
+SCHUR_ROWS = 1024
 PACK = 65
 
 
@@ -31,28 +31,43 @@
     ids_ref,
     row_ref,
     col_ref,
+    inverse_hbm,
+    couple_hbm,
+    block_hbm,
+    out_ref,
     inverse_ref,
     couple_ref,
-    block_hbm,
-    out_ref,
-    left_ref,
-    right_ref,
+    block_ref,
     ch_ref,
     cl_ref,
     sum_ref,
     uh_ref,
     ul_ref,
-    block_ref,
+    sems,
     block_sem,
-    *,
-    depths,
-    schurs,
 ):
+    outer = couple_ref.shape[1]
+    schurs = outer // SCHUR_ROWS
+    bounds = list(zip(CUTS[:-1], CUTS[1:]))
+
+    def fetches(n):
+        depth = slice(*bounds[n])
+        return [
+            pltpu.make_async_copy(couple_hbm.at[depth], couple_ref.at[depth], sems.at[n, 0]),
+            pltpu.make_async_copy(inverse_hbm.at[:, depth], inverse_ref.at[:, depth], sems.at[n, 1]),
+        ]
+
+    def start(n):
+        for fetch in fetches(n):
+            fetch.start()
+
     step = pl.program_id(0)
-    fetch = pltpu.make_async_copy(block_hbm, block_ref, block_sem)
+    fetch_block = pltpu.make_async_copy(block_hbm, block_ref, block_sem)
 
     @pl.when(step == 0)
     def _():
+        start(0)
+        start(1)
         lane = lax.broadcasted_iota(jnp.int32, (128, 128), 1)
         marks = jnp.zeros((128, 128), jnp.int32)
         for t in range(16):
@@ -62,84 +77,71 @@
             marks = jnp.where(lane == t, place, marks)
         out_ref[pl.ds(64, 128, stride=PACK), :] = marks.astype(jnp.float32)
 
-    def partial():
-        high, low = split(inverse_ref[...])
-        left_ref[:, :DEPTH] = high
-        left_ref[:, DEPTH : 2 * DEPTH] = low
-        left_ref[:, 2 * DEPTH :] = high
-        high, low = split(couple_ref[...])
-        right_ref[:DEPTH, :] = high
-        right_ref[DEPTH : 2 * DEPTH, :] = high
-        right_ref[2 * DEPTH :, :] = low
-        rows = pl.ds(step * DEPTH, DEPTH)
-        ch_ref[rows, :] = high
-        cl_ref[rows, :] = low
-        return dot(left_ref[...], right_ref[...], ((1,), (0,)))
-
-    @pl.when(step == 0)
-    def _():
-        sum_ref[...] = partial()
-
-    @pl.when((step > 0) & (step < depths - 1))
-    def _():
-        sum_ref[...] += partial()
-
-    @pl.when(step == 1)
-    def _():
-        fetch.start()
-
-    @pl.when(step == depths - 1)
-    def _():
-        uh_ref[...], ul_ref[...] = split(sum_ref[...] + partial())
-        fetch.wait()
-
+    def deepen(n):
+        for fetch in fetches(n):
+            fetch.wait()
+        if n + 2 < len(bounds):
+            start(n + 2)
+        elif n + 2 == len(bounds):
+            fetch_block.start()
+        depth = slice(*bounds[n])
+        ah, al = split(inverse_ref[:, depth])
+        ch, cl = split(couple_ref[depth, :])
+        ch_ref[depth, :] = ch
+        cl_ref[depth, :] = cl
+        across = ((1,), (0,))
+        product = dot(ah, ch, across) + (dot(ah, cl, across) + dot(al, ch, across))
+        if n == 0:
+            sum_ref[...] = product
+        elif n < len(bounds) - 1:
+            sum_ref[...] += product
+        else:
+            uh_ref[...], ul_ref[...] = split(sum_ref[...] + product)
+            fetch_block.wait()
+
+    def finish(part):
+        cols = slice(part * SCHUR_ROWS, (part + 1) * SCHUR_ROWS)
+        ch, cl, uh, ul = ch_ref[:, cols], cl_ref[:, cols], uh_ref[...], ul_ref[...]
+        across = ((0,), (0,))
+        schur = block_ref[cols, :] - (dot(ch, uh, across) + (dot(ch, ul, across) + dot(cl, uh, across)))
+        for n in range(SCHUR_ROWS // 128):
+            a, u = divmod(part * SCHUR_ROWS // 128 + n, 2)
+            for b in range(4):
+                for h in range(2):
+                    left = b * TILE + h * 128
+                    out_ref[pl.ds(pack_row(a, u, b, h), 128, stride=PACK), :] = schur[
+                        n * 128 : (n + 1) * 128, left : left + 128
+                    ]
+
+    for n in range(len(bounds)):
+        pl.when(step == n)(functools.partial(deepen, n))
     for part in range(schurs):
-
-        @pl.when(step == depths + part)
-        def _():
-            cols = slice(part * SCHUR_ROWS, (part + 1) * SCHUR_ROWS)
-            ch, cl, uh, ul = ch_ref[:, cols], cl_ref[:, cols], uh_ref[...], ul_ref[...]
-            across = ((0,), (0,))
-            schur = block_ref[cols, :] - (dot(ch, uh, across) + (dot(ch, ul, across) + dot(cl, uh, across)))
-            for n in range(SCHUR_ROWS // 128):
-                a, u = divmod(part * SCHUR_ROWS // 128 + n, 2)
-                for b in range(4):
-                    for h in range(2):
-                        left = b * TILE + h * 128
-                        out_ref[pl.ds(pack_row(a, u, b, h), 128, stride=PACK), :] = schur[
-                            n * 128 : (n + 1) * 128, left : left + 128
-                        ]
+        pl.when(step == len(bounds) + part)(functools.partial(finish, part))
 
 
 def schur_tiles(ids, row_place, col_place, inverse, couple, block):
     inner, outer = couple.shape
-    depths, schurs = inner // DEPTH, outer // SCHUR_ROWS
     smem = pl.BlockSpec(memory_space=pltpu.SMEM)
+    hbm = pl.BlockSpec(memory_space=pltpu.HBM)
     return pl.pallas_call(
-        functools.partial(schur_kernel, depths=depths, schurs=schurs),
-        grid=(depths + schurs,),
-        in_specs=[
-            smem,
-            smem,
-            smem,
-            pl.BlockSpec((inner, DEPTH), lambda s: (0, jnp.minimum(s, depths - 1))),
-            pl.BlockSpec((DEPTH, outer), lambda s: (jnp.minimum(s, depths - 1), 0)),
-            pl.BlockSpec(memory_space=pltpu.HBM),
-        ],
+        schur_kernel,
+        grid=(len(CUTS) - 1 + outer // SCHUR_ROWS,),
+        in_specs=[smem, smem, smem, hbm, hbm, hbm],
         out_specs=pl.BlockSpec(memory_space=pltpu.VMEM),
         out_shape=pltpu.VMEM((128 * PACK, 128), jnp.float32),
         scratch_shapes=[
-            pltpu.VMEM((inner, 3 * DEPTH), jnp.bfloat16),
-            pltpu.VMEM((3 * DEPTH, outer), jnp.bfloat16),
-            pltpu.VMEM((inner, outer), jnp.bfloat16),
-            pltpu.VMEM((inner, outer), jnp.bfloat16),
+            pltpu.VMEM((inner, inner), jnp.float32),
             pltpu.VMEM((inner, outer), jnp.float32),
-            pltpu.VMEM((inner, outer), jnp.bfloat16),
-            pltpu.VMEM((inner, outer), jnp.bfloat16),
             pltpu.VMEM((outer, outer), jnp.float32),
+            pltpu.VMEM((inner, outer), jnp.bfloat16),
+            pltpu.VMEM((inner, outer), jnp.bfloat16),
+            pltpu.VMEM((inner, outer), jnp.float32),
+            pltpu.VMEM((inner, outer), jnp.bfloat16),
+            pltpu.VMEM((inner, outer), jnp.bfloat16),
+            pltpu.SemaphoreType.DMA((len(CUTS) - 1, 2)),
             pltpu.SemaphoreType.DMA,
         ],
-        compiler_params=pltpu.CompilerParams(vmem_limit_bytes=56 * 1024 * 1024),
+        compiler_params=pltpu.CompilerParams(vmem_limit_bytes=57 * 1024 * 1024),
         cost_estimate=pl.CostEstimate(flops=24 * 10**9, bytes_accessed=25 * 10**6, transcendentals=0),
         name="schur",
     )(ids, row_place, col_place, inverse, couple, block)

time: 115 us -> 114 us (level)
  no operation moved by 1% of the time
where the time goes in v4:
time: 114 us
  blocking collectives  83.4 us (73%)
  Pallas kernels  29.6 us (26%)
    all_to_all x1, blocking collectives, on_device(): lax.all_to_all(pieces.reshape(128, PACK, 1, 128), AXES, 0, 0, tiled=True)  65.3 us
    pallas_call x1, Pallas kernels, schur_tiles(): pl.pallas_call(schur_kernel, grid=(len(CUTS) - 1 + outer // SCHUR_ROWS,),...  28.3 us
    all_to_all x1, blocking collectives, on_device(): owned = lax.all_to_all(total.reshape(128, 8, 128), AXES, 0, 0, tiled=True)  18.1 us

profile of v4, /device:TPU:1, one launch (start us, length us, event | category | flops | bytes accessed | tf_op | source)
XLA Modules:
  0.0 114.0 jit_solution(13020348535842021040)
XLA Ops:
  0.0 28.3 %schur.1 = f32[8320,128]{1,0:T(8,128)S(1)} custom-call(s32[4]{0:T(128)} %bitcast.18, s32[16]{0:T(128)} %row_ref.1, s32[16]{0:T(128)} %col_ref.1, f32[1536,1536]{1,0:T(8,128)} %bitcast.15, f32[1536,1024]{1,0:T(8,128)} %bitcast.16, f32[1024,1024]{1,0:T(8,128)} %bitcast.17), custom_call_target="tpu_custom_call" | custom-call | flops 24000000000 | bytes 25000000 | tf_op jit(solution)/shard_map/schur/pallas_call | solution.py:126
  28.3 65.3 %all_to_all.10 = f32[128,65,1,128]{3,2,1,0:T(1,128)S(1)} all-to-all(f32[128,65,1,128]{3,2,1,0:T(1,128)S(1)} %bitcast.12), channel_id=1, replica_groups=mesh['row'=8,'col'=16] {'row','col'}, dimensions={0} | all-to-all | bytes 8519680 | tf_op jit(solution)/shard_map/all_to_all | solution.py:188
  93.6 1.3 %combine.1 = f32[1024,128]{1,0:T(8,128)S(1)} custom-call(f32[8320,128]{1,0:T(8,128)S(1)} %bitcast.11), custom_call_target="tpu_custom_call" | custom-call | tf_op jit(solution)/shard_map/combine/pallas_call | solution.py:174
  94.9 18.1 %all_to_all.11 = f32[128,8,128]{2,1,0:T(8,128)S(1)} all-to-all(f32[128,8,128]{2,1,0:T(8,128)S(1)} %bitcast.13), channel_id=1, replica_groups=mesh['row'=8,'col'=16] {'row','col'}, dimensions={0} | all-to-all | bytes 1048576 | tf_op jit(solution)/shard_map/all_to_all | solution.py:190
  113.1 1.0 copy.10
